TPU v7x, 32 devices: a whole 2x2x4 slice. The times are simulated.
32 devices in a mesh: section: 2 (over y), ep: 16 (over z, x, core).
Axes of the slice: x: 2, y: 2, z: 4, core: 2. Of those that a mesh axis runs over, the one named last changes fastest.
Arguments:
- inputs: bfloat16 [2, 2048, 1536], P('section', 'ep'), may hold values from -6 to 6
- upstream: bfloat16 [2, 2048, 1536], P('section', 'ep'), may hold values from -6 to 6
- gate_saved: bfloat16 [2, 2048, 8, 384], P('section', 'ep'), may hold values from -6 to 6
- expert_ids: int32 [2, 2048, 8], P('section', 'ep'), may hold values from 0 to 31, all different within a row; in each aligned block of 128 rows (0 to 127, 128 to 255, ..., all dimensions but the last counted through in order) at most 48 rows name the same one
- route_weights: float32 [2, 2048, 8], P('section', 'ep'), may hold values from 0.05 to 0.5
- w_up: bfloat16 [2, 32, 1536, 384], P('section', 'ep'), may hold values from -0.15625 to 0.15625
- w_down: bfloat16 [2, 32, 384, 1536], P('section', 'ep'), may hold values from -0.3125 to 0.3125
Outputs:
- delivered: bfloat16 [2, 2048, 1536], P('section', 'ep')
- grad_up: bfloat16 [2, 32, 1536, 384], P('section', 'ep')
- grad_down: bfloat16 [2, 32, 384, 1536], P('section', 'ep')
Inputs may be any that keep to these rules, and one draw needn't show every extreme that they name: `expert_ids`: each row names 8 different experts. In the rows of one device no expert is named more than 48 times, and in every draw some expert is named exactly 48 times in the rows of some device; every expert is named somewhere.
All inputs are finite; a program needn't handle non-finite values.
Results may differ from a plain program's by a relative error of at most 0.012.
Values may be sent and summed in bfloat16 or wider, within the bound.
A program may use at most 192 MiB of HBM per device.

v0:
```python
import jax
import jax.numpy as jnp
from jax import lax
from jax.sharding import PartitionSpec as P

BF16 = jnp.bfloat16
F32 = jnp.float32


def from_behind(block, axis, distance):
    devices = range(lax.axis_size(axis))
    route = [((i - distance) % len(devices), i) for i in devices]
    return lax.ppermute(block, axis, route)


def body(inputs, upstream, gate_saved, expert_ids, route_weights, w_up, w_down):
    ep = lax.axis_size("ep")
    local = w_up.shape[1]
    experts = local * ep
    toks, top = expert_ids.shape[1:]
    cap = 3 * toks * top // (2 * experts)
    width = inputs.shape[2]
    ff = w_up.shape[3]
    routing = jnp.concatenate([expert_ids[0].astype(F32), route_weights[0]], axis=1)
    routing_all = lax.all_gather(routing, "ep", axis=0, tiled=False)
    ids = expert_ids[0]
    hit = ids[:, :, None] == jnp.arange(experts, dtype=jnp.int32)
    member = jnp.any(hit, axis=1).astype(BF16)
    lower = (jnp.arange(toks)[:, None] > jnp.arange(toks)[None, :]).astype(BF16)
    rank = jnp.dot(lower, member, preferred_element_type=F32)
    place = jnp.sum(jnp.where(hit, rank[:, None, :], 0.0), axis=2)
    slot = (ids * cap + place.astype(jnp.int32)).reshape(1, toks * top)
    pick = (jnp.arange(experts * cap, dtype=jnp.int32)[:, None] == slot).astype(BF16)
    gate_send = jnp.dot(pick, gate_saved[0].reshape(toks * top, ff), preferred_element_type=F32)
    gate_send = gate_send.astype(BF16).reshape(ep, local, cap, ff)
    gate_recv = lax.all_to_all(gate_send, "ep", split_axis=0, concat_axis=0, tiled=True)
    cot = from_behind(upstream, "section", -1)[0]
    x_all = lax.all_gather(inputs[0], "ep", axis=0, tiled=True)
    c_all = lax.all_gather(cot, "ep", axis=0, tiled=True)
    me = lax.axis_index("ep")
    mine = (me * local + jnp.arange(local)).astype(F32)
    hits = routing_all[:, :, :top, None] == mine
    weight = jnp.sum(jnp.where(hits, routing_all[:, :, top:, None], 0.0), axis=2)
    members = jnp.any(hits, axis=2)
    ranks = jnp.einsum("ab,sbe->sae", lower, members.astype(BF16), preferred_element_type=F32)
    ranks = jnp.where(members, ranks, -1.0)
    spread = (ranks[:, :, :, None] == jnp.arange(cap).astype(F32)).astype(BF16)
    gate = jnp.einsum("stec,secf->stef", spread, gate_recv, preferred_element_type=F32)
    act = jax.nn.silu(gate).reshape(ep * toks, local, ff)
    weight = weight.reshape(ep * toks, local, 1)
    act_w = act * weight
    up = w_up[0]
    down = w_down[0]
    up_cat = jnp.transpose(up, (1, 0, 2)).reshape(width, local * ff)
    down_cat = down.reshape(local * ff, width)
    act_w = act_w.reshape(ep * toks, local * ff)
    u = jnp.dot(x_all, up_cat, preferred_element_type=F32)
    hidden = (act_w * u).astype(BF16)
    h = lax.dot_general(c_all, down_cat, (((1,), (1,)), ((), ())), preferred_element_type=F32)
    g = (act_w * h).astype(BF16)
    part = lax.dot_general(g, up_cat, (((1,), (1,)), ((), ())), preferred_element_type=F32)
    grad = lax.psum_scatter(part.astype(BF16), "ep", scatter_dimension=0, tiled=True)
    delivered = from_behind(grad[None], "section", -1)
    grad_down = lax.dot_general(hidden, c_all, (((0,), (0,)), ((), ())), preferred_element_type=F32)
    grad_up = jnp.stack(
        [
            lax.dot_general(
                x_all,
                g[:, e * ff : (e + 1) * ff],
                (((0,), (0,)), ((), ())),
                preferred_element_type=F32,
            )
            for e in range(local)
        ]
    )
    return (
        delivered,
        grad_up.astype(BF16)[None],
        grad_down.astype(BF16).reshape(1, local, ff, width),
    )


def solution(mesh):
    return jax.shard_map(
        body,
        mesh=mesh,
        in_specs=(
            P("section", "ep", None),
            P("section", "ep", None),
            P("section", "ep", None, None),
            P("section", "ep", None),
            P("section", "ep", None),
            P("section", "ep", None, None),
            P("section", "ep", None, None),
        ),
        out_specs=(
            P("section", "ep", None),
            P("section", "ep", None, None),
            P("section", "ep", None, None),
        ),
        check_vma=False,
    )
```

profile of v0, /device:TPU:0, one launch (start us, length us, event | category | flops | bytes accessed | tf_op | source)
XLA Modules:
  0.0 272.7 jit_solution(5686237098454286970)
XLA Ops:
  7.2 0.0 copy-start
  7.2 0.0 all-gather.6.cloned.1.call-start
  7.2 3.1 %collective-permute-start = (bf16[1,128,1536]{2,1,0:T(8,128)(2,1)}, bf16[1,128,1536]{2,1,0:T(8,128)(2,1)S(1)}, u32[]{:S(2)}, u32[]{:S(2)}) collective-permute-start(bf16[1,128,1536]{2,1,0:T(8,128)(2,1)} %param.8), channel_id=1, source_target_pairs={{16,0},{0,16},{17,1},{1,17},{18,2},{2,18},{19,3},{3,19},{20,4},{4,... | collective-permute-start | bytes 1179656 | tf_op jit(solution)/shard_map/ppermute | solution.py:13
  10.3 9.3 %collective-permute-done = bf16[1,128,1536]{2,1,0:T(8,128)(2,1)S(1)} collective-permute-done((bf16[1,128,1536]{2,1,0:T(8,128)(2,1)}, bf16[1,128,1536]{2,1,0:T(8,128)(2,1)S(1)}, u32[]{:S(2)}, u32[]{:S(2)}) %collective-permute-start) | collective-permute-done | bytes 393248 | tf_op jit(solution)/shard_map/ppermute | solution.py:13
  19.6 0.0 copy-start.4
  19.6 0.7 copy-done.4
  20.4 0.0 all-gather.6.cloned.1.call-update
  20.4 0.0 all-gather.8.cloned.1.call-start
  20.4 0.7 all-gather.8.cloned.1.call-update
  21.1 0.7 bitcast_convert_fusion
  21.8 0.1 copy.35
  21.9 0.1 mul.41
  22.0 0.7 fusion.45
  22.7 0.1 fusion.47
  22.9 0.7 select_reduce_fusion
  23.6 0.1 copy.36
  23.7 0.1 convert_element_type.56
  23.8 0.0 copy-start.5
  23.8 4.0 %fusion.22 = bf16[1536,384]{1,0:T(8,128)(2,1)} fusion(s32[1024]{0:T(1024)S(1)} %add.23, bf16[1,128,8,384]{3,2,1,0:T(8,128)(2,1)} %param.9), kind=kOutput, calls=%fused_computation.22 | convolution fusion | flops 1210122240 | bytes 1970176 | tf_op jit(solution)/shard_map/dot_general | solution.py:34
  27.8 6.2 %all-to-all-start = ((bf16[16,2,48,384]{3,2,1,0:T(8,128)(2,1)}), bf16[16,2,48,384]{3,2,1,0:T(8,128)(2,1)}, u32[]{:S(2)}, u32[]{:S(2)}) async-start(bf16[16,2,48,384]{3,2,1,0:T(8,128)(2,1)} %bitcast.2), calls=%async_computation | async-start | bytes 2359296 | tf_op jit(solution)/shard_map/all_to_all | solution.py:36
  34.0 0.0 reduce-scatter.2.cloned.1.call-start
  34.0 0.0 copy-done.5
  34.0 45.0 %all-gather = f32[2048,16]{0,1:T(8,128)S(1)} all-gather(f32[128,16]{0,1:T(8,128)S(1)} %pad_maximum_fusion.1), channel_id=2, replica_groups=mesh['section'=2,'ep'=16] {'ep'}, dimensions={0}, use_global_device_ids=true | all-gather | bytes 139264 | tf_op jit(solution)/shard_map/all_gather | solution.py:25
  79.1 0.1 compare_reduce_fusion
  79.2 0.1 fusion.37
  79.4 0.1 fusion.44
  79.6 0.4 copy.43
  79.9 4.8 %mul.45 = f32[2048,2,384]{2,1,0:T(2,128)S(1)} broadcast(f32[2048,2]{1,0:T(8,128)S(1)} %copy.43), dimensions={0,1} | broadcast | bytes 6307840 | tf_op jit(solution)/shard_map/mul | solution.py:51
  84.8 3.0 %copy.53 = f32[256,8,2,384]{3,1,2,0:T(8,128)} copy(f32[256,8,2,384]{3,2,1,0:T(2,128)S(1)} %bitcast.86) | data formatting | bytes 12582912
  87.8 4.3 %copy.45 = bf16[1,2,1536,384]{2,3,1,0:T(8,128)(2,1)} copy(bf16[1,2,1536,384]{3,2,1,0:T(8,128)(2,1)} %param.12) | data formatting | bytes 4718592 | tf_op args[5]
  92.1 0.0 all-to-all-done
  92.1 5.8 %bitcast_multiply_fusion = f32[16,128,2,384]{1,3,2,0:T(8,128)} fusion(bf16[16,2,48,384]{3,2,1,0:T(8,128)(2,1)} %all-to-all-done, f32[16,128,2]{1,2,0:T(2,128)S(1)} %copy.40, f32[48]{0:T(128)S(1)} %iota_convert_fusion), kind=kOutput, calls=%fused_computation.11 | convolution fusion | flops 157483008 | bytes 7487680 | tf_op jit(solution)/shard_map/stec,secf->stef/dot_general | solution.py:48
  97.8 10.3 %copy.47 = f32[16,128,2,384]{3,2,1,0:T(2,128)} copy(f32[16,128,2,384]{1,3,2,0:T(8,128)} %bitcast_multiply_fusion) | data formatting | bytes 12582912 | tf_op jit(solution)/shard_map/reshape | solution.py:49
  108.2 6.1 %copy.52 = f32[256,8,2,384]{3,1,2,0:T(8,128)} copy(f32[256,8,2,384]{3,2,1,0:T(2,128)} %bitcast.87) | data formatting | bytes 12582912
  114.2 0.0 all-gather.6.cloned.1.call-done
  114.2 0.0 copy-done
  114.2 0.0 copy-start.2
  114.2 10.2 %multiply_convert_fusion.1 = bf16[2048,768]{1,0:T(8,128)(2,1)S(1)} fusion(bf16[768,1536]{1,0:T(8,128)(2,1)S(1)} %bitcast.85, bf16[1,2048,1536]{2,1,0:T(8,128)(2,1)} %all-gather.6.cloned.1.call-done, f32[2048,768]{1,0:T(8,128)} %bitcast.90, f32[2048,768]{1,0:T(8,128)} %bitcast.88), kind=kOutput, calls=%fused_computation.17 | convolution fusion | flops 4836556800 | bytes 24379392 | tf_op jit(solution)/shard_map/dot_general | solution.py:59
  124.5 0.0 copy-start.6
  124.5 1.6 copy-done.6
  126.1 0.0 copy-done.2
  126.1 6.9 %convolution_convert_fusion = bf16[2048,1536]{1,0:T(8,128)(2,1)} fusion(bf16[2048,768]{1,0:T(8,128)(2,1)S(1)} %multiply_convert_fusion.1, bf16[1536,768]{0,1:T(8,128)(2,1)S(1)} %bitcast.92), kind=kOutput, calls=%fused_computation | convolution fusion | flops 4834983936 | bytes 11796480 | tf_op jit(solution)/shard_map/dot_general | solution.py:61
  133.0 0.0 reduce-scatter.2.cloned.1.call-update
  133.1 0.0 copy-start.3
  133.1 30.3 %all-gather.8.cloned.1.call-done = bf16[1,2048,1536]{2,1,0:T(8,128)(2,1)} async-done(((bf16[1,128,1536]{2,1,0:T(8,128)(2,1)}), bf16[1,2048,1536]{2,1,0:T(8,128)(2,1)}) %all-gather.8.cloned.1.call-update) | async-done | bytes 6291472 | tf_op jit(solution)/shard_map/all_gather | solution.py:38
  163.4 5.9 %fusion.29 = bf16[1,1,1536,384]{2,3,1,0:T(8,128)(2,1)S(1)} fusion(bf16[1,2048,1536]{2,1,0:T(8,128)(2,1)} %all-gather.8.cloned.1.call-done, bf16[2048,768]{1,0:T(8,128)(2,1)} %copy-done.6), kind=kOutput, calls=%fused_computation.25 | convolution fusion | flops 2416508928 | bytes 9043968 | tf_op jit(solution)/shard_map/dot_general | solution.py:67
  169.3 0.0 copy-done.3
  169.3 30.7 %fusion.18 = bf16[768,1536]{1,0:T(8,128)(2,1)} fusion(bf16[1,2048,1536]{2,1,0:T(8,128)(2,1)} %all-gather.6.cloned.1.call-done, bf16[1536,768]{0,1:T(8,128)(2,1)S(1)} %bitcast.93, bf16[1,2048,1536]{2,1,0:T(8,128)(2,1)} %all-gather.8.cloned.1.call-done, f32[2048,768]{1,0:T(8,128)} %bitcast.91, f32[2048,768]{1,0:T(8,128)} %bitcast.89), kind=kOutput, calls=%fused_computation.20 | convolution fusion | flops 9669574656 | bytes 29884416 | tf_op jit(solution)/shard_map/dot_general | solution.py:64
  200.0 51.1 %reduce-scatter.2.cloned.1.call-done = bf16[128,1536]{1,0:T(8,128)(2,1)} async-done(((bf16[2048,1536]{1,0:T(8,128)(2,1)}), bf16[128,1536]{1,0:T(8,128)(2,1)}) %reduce-scatter.2.cloned.1.call-update) | async-done | bytes 393232 | tf_op jit(solution)/shard_map/reduce_scatter | solution.py:62
  251.1 1.5 collective-permute-start.1
  252.6 5.9 %fusion.32 = bf16[1,1,1536,384]{2,3,1,0:T(8,128)(2,1)S(1)} fusion(bf16[1,2048,1536]{2,1,0:T(8,128)(2,1)} %all-gather.8.cloned.1.call-done, bf16[2048,768]{1,0:T(8,128)(2,1)} %copy-done.6), kind=kOutput, calls=%fused_computation.26 | convolution fusion | flops 2416508928 | bytes 9043968 | tf_op jit(solution)/shard_map/dot_general | solution.py:67
  258.5 0.0 copy-start.1
  258.5 1.6 pad_maximum_fusion
  260.2 4.3 %copy.46 = bf16[1,2,1536,384]{3,2,1,0:T(8,128)(2,1)} copy(bf16[1,2,1536,384]{2,3,1,0:T(8,128)(2,1)} %pad_maximum_fusion) | data formatting | bytes 4718592
  264.4 0.0 collective-permute-done.1
  264.4 1.8 copy.57
  266.2 0.0 copy-done.1
  (10 shorter events, 0.1 us)
Async XLA Ops:
  7.2 107.1 %copy-start = (bf16[1,2,384,1536]{3,2,1,0:T(8,128)(2,1)S(1)}, bf16[1,2,384,1536]{3,2,1,0:T(8,128)(2,1)}, u32[]{:S(2)}) copy-start(bf16[1,2,384,1536]{3,2,1,0:T(8,128)(2,1)} %param.13) | copy-start | bytes 7077892
  7.2 107.1 %all-gather.6.cloned.1.call-start = ((), (), s32[]{:S(2)}) async-start(), calls=%async_computation.3 | async-start | bytes 6684672 | tf_op jit(solution)/shard_map/all_gather | solution.py:39
  7.2 12.4 %collective-permute-start = (bf16[1,128,1536]{2,1,0:T(8,128)(2,1)}, bf16[1,128,1536]{2,1,0:T(8,128)(2,1)S(1)}, u32[]{:S(2)}, u32[]{:S(2)}) collective-permute-start(bf16[1,128,1536]{2,1,0:T(8,128)(2,1)} %param.8), channel_id=1, source_target_pairs={{16,0},{0,16},{17,1},{1,17},{18,2},{2,18},{19,3},{3,19},{20,4},{4,... | collective-permute-start | bytes 1179656 | tf_op jit(solution)/shard_map/ppermute | solution.py:13
  19.6 0.7 copy-start.4
  20.4 143.0 %all-gather.8.cloned.1.call-start = ((), (), s32[]{:S(2)}) async-start(), calls=%async_computation.4 | async-start | bytes 6684672 | tf_op jit(solution)/shard_map/all_gather | solution.py:38
  23.8 10.2 %copy-start.5 = (f32[1,128,8]{1,2,0:T(8,128)S(1)}, f32[1,128,8]{1,2,0:T(8,128)}, u32[]{:S(2)}) copy-start(f32[1,128,8]{1,2,0:T(8,128)} %param.11) | copy-start | bytes 12292
  27.8 64.3 %all-to-all-start = ((bf16[16,2,48,384]{3,2,1,0:T(8,128)(2,1)}), bf16[16,2,48,384]{3,2,1,0:T(8,128)(2,1)}, u32[]{:S(2)}, u32[]{:S(2)}) async-start(bf16[16,2,48,384]{3,2,1,0:T(8,128)(2,1)} %bitcast.2), calls=%async_computation | async-start | bytes 2359296 | tf_op jit(solution)/shard_map/all_to_all | solution.py:36
  34.0 217.2 %reduce-scatter.2.cloned.1.call-start = ((), (), s32[]{:S(2)}) async-start(), calls=%async_computation.2 | async-start | bytes 6684672 | tf_op jit(solution)/shard_map/reduce_scatter | solution.py:62
  114.2 11.9 %copy-start.2 = (bf16[1,2,1536,384]{2,3,1,0:T(8,128)(2,1)S(1)}, bf16[1,2,1536,384]{2,3,1,0:T(8,128)(2,1)}, u32[]{:S(2)}) copy-start(bf16[1,2,1536,384]{2,3,1,0:T(8,128)(2,1)} %copy.45) | copy-start | bytes 7077892
  124.5 1.6 copy-start.6
  133.1 36.2 %copy-start.3 = (bf16[1,2,1536,384]{2,3,1,0:T(8,128)(2,1)S(1)}, bf16[1,2,1536,384]{2,3,1,0:T(8,128)(2,1)}, u32[]{:S(2)}) copy-start(bf16[1,2,1536,384]{2,3,1,0:T(8,128)(2,1)} %copy.45) | copy-start | bytes 7077892
  251.1 13.3 %collective-permute-start.1 = (bf16[1,128,1536]{2,1,0:T(8,128)(2,1)}, bf16[1,128,1536]{2,1,0:T(8,128)(2,1)}, u32[]{:S(2)}, u32[]{:S(2)}) collective-permute-start(bf16[1,128,1536]{2,1,0:T(8,128)(2,1)} %bitcast.100), channel_id=1, source_target_pairs={{16,0},{0,16},{17,1},{1,17},{18,2},{2,18},{19,3},{3,19},{20,4},{4,... | collective-permute-start | bytes 1179656 | tf_op jit(solution)/shard_map/ppermute | solution.py:13
  258.5 7.7 %copy-start.1 = (bf16[1,2,384,1536]{3,2,1,0:T(8,128)(2,1)S(1)}, bf16[1,2,384,1536]{3,2,1,0:T(8,128)(2,1)}, u32[]{:S(2)}) copy-start(bf16[1,2,384,1536]{3,2,1,0:T(8,128)(2,1)} %param.13) | copy-start | bytes 7077892
Sparse Core Ops, SparseCore 0:
  20.5 80.3 all-gather.5
  103.2 60.1 all-gather.7
  167.3 83.7 reduce-scatter.1
where the time goes:
time: 274 us; the launch traced here: 273 us
  waiting for transfers between devices  91.5 us (33%)
  matrix products  69.7 us (25%)
  blocking collectives  45 us (16%)
  local copies, waits for them, and re-layouts  37.8 us (14%)
  between operations  13.9 us (5%)
  starting transfers between devices  10.8 us (4%)
  other arithmetic  4 us (1%)
    reduce_scatter x1, waiting for transfers between devices, body(): lax.psum_scatter(part.astype(BF16), 'ep', scatter_dimension=0, tiled=True)  51.1 us
    all_gather x1, blocking collectives, body(): routing_all = lax.all_gather(routing, 'ep', axis=0, tiled=False)  45 us
    dot_general x1, matrix products, body(): lax.dot_general(hidden, c_all, (((0,), (0,)), ((), ())), preferred_elemen...  30.7 us
    all_gather x1, waiting for transfers between devices, body(): x_all = lax.all_gather(inputs[0], 'ep', axis=0, tiled=True)  30.3 us
    unnamed x22, local copies, waits for them, and re-layouts  21.9 us
    dot_general x2, matrix products, body(): lax.dot_general(x_all, g[:, e * ff:(e + 1) * ff], (((0,), (0,)), ((), ())...  11.8 us
    reshape x1, local copies, waits for them, and re-layouts, body(): act = jax.nn.silu(gate).reshape(ep * toks, local, ff)  10.3 us
    dot_general x1, matrix products, body(): lax.dot_general(c_all, down_cat, (((1,), (1,)), ((), ())), preferred_elem...  10.2 us
  transfers between devices with their start and end apart: 6, of which 3 were waited for; matrix products, arithmetic and copies ran while one was open for 39% of the time, Pallas kernels for 0%

commit v1 on v0

--- a/solution.py
+++ b/solution.py
@@ -35,7 +35,16 @@
     gate_send = gate_send.astype(BF16).reshape(ep, local, cap, ff)
     gate_recv = lax.all_to_all(gate_send, "ep", split_axis=0, concat_axis=0, tiled=True)
     cot = from_behind(upstream, "section", -1)[0]
-    x_all = lax.all_gather(inputs[0], "ep", axis=0, tiled=True)
+    panel = inputs[0]
+    cores_n = jax.lax.axis_size("ep")
+    nodes = [(p, (p + 1) % cores_n) for p in range(cores_n)]
+    left_arr = [None] * cores_n
+    left_arr[cores_n - 1] = panel
+    for dev in range(cores_n - 2, -1, -1):
+        left_arr[dev] = jax.lax.ppermute(left_arr[dev + 1], "ep", nodes)
+    v1 = jnp.concatenate(left_arr, 0)
+    view_out = (jax.lax.axis_index("ep") + 1) * panel.shape[0]
+    x_all = jnp.roll(v1, view_out, 0)
     c_all = lax.all_gather(cot, "ep", axis=0, tiled=True)
     me = lax.axis_index("ep")
     mine = (me * local + jnp.arange(local)).astype(F32)

time: 274 us -> 380 us (1.39)
  waiting for transfers between devices: 91.5 us -> 178 us
  local copies, waits for them, and re-layouts: 37.8 us -> 79 us
  blocking collectives: 45 us -> 20 us
    ppermute x0 -> x15, waiting for transfers between devices: none -> 147 us  [body(): left_arr[dev] = jax.lax.ppermute(left_arr[dev + 1], 'ep', nodes)]
    unnamed x22 -> x100, local copies, waits for them, and re-layouts: 21.9 us -> 60.9 us
    reduce_scatter x1, waiting for transfers between devices: 51.1 us -> 20.6 us  [body(): lax.psum_scatter(part.astype(BF16), 'ep', scatter_dimension=0, tiled=True)]
    all_gather x1 -> x0, waiting for transfers between devices: 30.3 us -> none  [body(): x_all = lax.all_gather(inputs[0], 'ep', axis=0, tiled=True)]
    all_gather x1, blocking collectives: 45 us -> 20 us  [body(): routing_all = lax.all_gather(routing, 'ep', axis=0, tiled=False)]
  transfers between devices with their start and end apart: 6 -> 20, of which waited for: 3 -> 14; matrix products, arithmetic and copies ran while one was open for 39% -> 34% of each run, Pallas kernels for 0% -> 0%
where the time goes in v1:
time: 380 us; the launch traced here: 378 us
  waiting for transfers between devices  178 us (47%)
  local copies, waits for them, and re-layouts  79 us (21%)
  matrix products  70.2 us (18%)
  blocking collectives  20 us (5%)
  between operations  14.3 us (4%)
  starting transfers between devices  11.2 us (3%)
  other arithmetic  5.74 us (2%)
    ppermute x15, waiting for transfers between devices, body(): left_arr[dev] = jax.lax.ppermute(left_arr[dev + 1], 'ep', nodes)  147 us
    unnamed x100, local copies, waits for them, and re-layouts  60.9 us
    dot_general x1, matrix products, body(): lax.dot_general(hidden, c_all, (((0,), (0,)), ((), ())), preferred_elemen...  29.3 us
    reduce_scatter x1, waiting for transfers between devices, body(): lax.psum_scatter(part.astype(BF16), 'ep', scatter_dimension=0, tiled=True)  20.6 us
    all_gather x1, blocking collectives, body(): routing_all = lax.all_gather(routing, 'ep', axis=0, tiled=False)  20 us
    dot_general x2, matrix products, body(): lax.dot_general(x_all, g[:, e * ff:(e + 1) * ff], (((0,), (0,)), ((), ())...  13.6 us
    reshape x1, local copies, waits for them, and re-layouts, body(): act = jax.nn.silu(gate).reshape(ep * toks, local, ff)  10.4 us
    dot_general x1, matrix products, body(): lax.dot_general(c_all, down_cat, (((1,), (1,)), ((), ())), preferred_elem...  10.2 us
  transfers between devices with their start and end apart: 20, of which 14 were waited for; matrix products, arithmetic and copies ran while one was open for 34% of the time, Pallas kernels for 0%

profile of v1, /device:TPU:0, one launch (start us, length us, event | category | flops | bytes accessed | tf_op | source)
XLA Modules:
  0.0 378.2 jit_solution(10983888891899841626)
XLA Ops:
  7.2 3.1 collective-permute-start
  10.3 9.3 %collective-permute-done = bf16[1,128,1536]{2,1,0:T(8,128)(2,1)S(1)} collective-permute-done((bf16[1,128,1536]{2,1,0:T(8,128)(2,1)}, bf16[1,128,1536]{2,1,0:T(8,128)(2,1)S(1)}, u32[]{:S(2)}, u32[]{:S(2)}) %collective-permute-start) | collective-permute-done | bytes 393248 | tf_op jit(solution)/shard_map/ppermute | solution.py:13
  20.5 10.1 %collective-permute-done.2 = bf16[128,1536]{1,0:T(8,128)(2,1)S(1)} collective-permute-done((bf16[128,1536]{1,0:T(8,128)(2,1)}, bf16[128,1536]{1,0:T(8,128)(2,1)S(1)}, u32[]{:S(2)}, u32[]{:S(2)}) %collective-permute-start.2) | collective-permute-done | bytes 393248 | tf_op jit(solution)/shard_map/ppermute | solution.py:44
  31.3 18.3 %collective-permute-done.3 = bf16[128,1536]{1,0:T(8,128)(2,1)S(1)} collective-permute-done((bf16[128,1536]{1,0:T(8,128)(2,1)S(1)}, bf16[128,1536]{1,0:T(8,128)(2,1)S(1)}, u32[]{:S(2)}, u32[]{:S(2)}) %collective-permute-start.3) | collective-permute-done | bytes 393248 | tf_op jit(solution)/shard_map/ppermute | solution.py:44
  50.3 10.1 %collective-permute-done.4 = bf16[128,1536]{1,0:T(8,128)(2,1)S(1)} collective-permute-done((bf16[128,1536]{1,0:T(8,128)(2,1)S(1)}, bf16[128,1536]{1,0:T(8,128)(2,1)S(1)}, u32[]{:S(2)}, u32[]{:S(2)}) %collective-permute-start.4) | collective-permute-done | bytes 393248 | tf_op jit(solution)/shard_map/ppermute | solution.py:44
  61.2 18.4 %collective-permute-done.5 = bf16[128,1536]{1,0:T(8,128)(2,1)S(1)} collective-permute-done((bf16[128,1536]{1,0:T(8,128)(2,1)S(1)}, bf16[128,1536]{1,0:T(8,128)(2,1)S(1)}, u32[]{:S(2)}, u32[]{:S(2)}) %collective-permute-start.5) | collective-permute-done | bytes 393248 | tf_op jit(solution)/shard_map/ppermute | solution.py:44
  80.4 17.0 %collective-permute-done.6 = bf16[128,1536]{1,0:T(8,128)(2,1)S(1)} collective-permute-done((bf16[128,1536]{1,0:T(8,128)(2,1)S(1)}, bf16[128,1536]{1,0:T(8,128)(2,1)S(1)}, u32[]{:S(2)}, u32[]{:S(2)}) %collective-permute-start.6) | collective-permute-done | bytes 393248 | tf_op jit(solution)/shard_map/ppermute | solution.py:44
  98.1 9.9 %collective-permute-done.7 = bf16[128,1536]{1,0:T(8,128)(2,1)S(1)} collective-permute-done((bf16[128,1536]{1,0:T(8,128)(2,1)S(1)}, bf16[128,1536]{1,0:T(8,128)(2,1)S(1)}, u32[]{:S(2)}, u32[]{:S(2)}) %collective-permute-start.7) | collective-permute-done | bytes 393248 | tf_op jit(solution)/shard_map/ppermute | solution.py:44
  109.5 9.2 %collective-permute-done.8 = bf16[128,1536]{1,0:T(8,128)(2,1)S(1)} collective-permute-done((bf16[128,1536]{1,0:T(8,128)(2,1)S(1)}, bf16[128,1536]{1,0:T(8,128)(2,1)S(1)}, u32[]{:S(2)}, u32[]{:S(2)}) %collective-permute-start.8) | collective-permute-done | bytes 393248 | tf_op jit(solution)/shard_map/ppermute | solution.py:44
  120.6 7.9 %collective-permute-done.9 = bf16[128,1536]{1,0:T(8,128)(2,1)S(1)} collective-permute-done((bf16[128,1536]{1,0:T(8,128)(2,1)S(1)}, bf16[128,1536]{1,0:T(8,128)(2,1)S(1)}, u32[]{:S(2)}, u32[]{:S(2)}) %collective-permute-start.9) | collective-permute-done | bytes 393248 | tf_op jit(solution)/shard_map/ppermute | solution.py:44
  128.6 4.1 %fusion.28 = bf16[1536,384]{1,0:T(8,128)(2,1)} fusion(s32[1024]{0:T(1024)S(1)} %add.36, bf16[1,128,8,384]{3,2,1,0:T(8,128)(2,1)} %param.9), kind=kOutput, calls=%fused_computation.24 | convolution fusion | flops 1210122240 | bytes 1970176 | tf_op jit(solution)/shard_map/dot_general | solution.py:34
  132.7 5.7 %all-to-all-start = ((bf16[16,2,48,384]{3,2,1,0:T(8,128)(2,1)}), bf16[16,2,48,384]{3,2,1,0:T(8,128)(2,1)}, u32[]{:S(2)}, u32[]{:S(2)}) async-start(bf16[16,2,48,384]{3,2,1,0:T(8,128)(2,1)} %bitcast.75), calls=%async_computation | async-start | bytes 2359296 | tf_op jit(solution)/shard_map/all_to_all | solution.py:36
  138.9 28.7 %collective-permute-done.11 = bf16[128,1536]{1,0:T(8,128)(2,1)S(1)} collective-permute-done((bf16[128,1536]{1,0:T(8,128)(2,1)S(1)}, bf16[128,1536]{1,0:T(8,128)(2,1)S(1)}, u32[]{:S(2)}, u32[]{:S(2)}) %collective-permute-start.11) | collective-permute-done | bytes 393248 | tf_op jit(solution)/shard_map/ppermute | solution.py:44
  168.4 10.0 %collective-permute-done.12 = bf16[128,1536]{1,0:T(8,128)(2,1)} collective-permute-done((bf16[128,1536]{1,0:T(8,128)(2,1)S(1)}, bf16[128,1536]{1,0:T(8,128)(2,1)}, u32[]{:S(2)}, u32[]{:S(2)}) %collective-permute-start.12) | collective-permute-done | bytes 393248 | tf_op jit(solution)/shard_map/ppermute | solution.py:44
  178.4 20.0 %all-gather = f32[2048,16]{0,1:T(8,128)S(1)} all-gather(f32[128,16]{0,1:T(8,128)S(1)} %pad_maximum_fusion.1), channel_id=2, replica_groups=mesh['section'=2,'ep'=16] {'ep'}, dimensions={0}, use_global_device_ids=true | all-gather | bytes 139264 | tf_op jit(solution)/shard_map/all_gather | solution.py:25
  200.1 1.0 compare_reduce_fusion
  201.0 7.6 %collective-permute-done.14 = bf16[128,1536]{1,0:T(8,128)(2,1)} collective-permute-done((bf16[128,1536]{1,0:T(8,128)(2,1)}, bf16[128,1536]{1,0:T(8,128)(2,1)}, u32[]{:S(2)}, u32[]{:S(2)}) %collective-permute-start.14) | collective-permute-done | bytes 393248 | tf_op jit(solution)/shard_map/ppermute | solution.py:44
  209.4 0.9 copy.46
  210.3 1.0 fusion.44
  211.7 4.8 %mul.48 = f32[2048,2,384]{2,1,0:T(2,128)S(1)} broadcast(f32[2048,2]{1,0:T(8,128)S(1)} %copy.40), dimensions={0,1} | broadcast | bytes 6307840 | tf_op jit(solution)/shard_map/mul | solution.py:60
  216.5 3.1 copy.49
  219.6 4.3 %copy.42 = bf16[1,2,1536,384]{2,3,1,0:T(8,128)(2,1)} copy(bf16[1,2,1536,384]{3,2,1,0:T(8,128)(2,1)} %param.12) | data formatting | bytes 4718592 | tf_op args[5]
  223.9 5.8 %bitcast_multiply_fusion = f32[16,128,2,384]{1,3,2,0:T(8,128)} fusion(bf16[16,2,48,384]{3,2,1,0:T(8,128)(2,1)} %all-to-all-done, f32[16,128,2]{1,2,0:T(2,128)S(1)} %copy-done.27, f32[48]{0:T(128)S(1)} %iota_convert_fusion), kind=kOutput, calls=%fused_computation.5 | convolution fusion | flops 157483008 | bytes 7487680 | tf_op jit(solution)/shard_map/stec,secf->stef/dot_general | solution.py:57
  229.7 10.4 %copy.43 = f32[16,128,2,384]{3,2,1,0:T(2,128)} copy(f32[16,128,2,384]{1,3,2,0:T(8,128)} %bitcast_multiply_fusion) | data formatting | bytes 12582912 | tf_op jit(solution)/shard_map/reshape | solution.py:58
  240.1 5.9 %copy.48 = f32[256,8,2,384]{3,1,2,0:T(8,128)} copy(f32[256,8,2,384]{3,2,1,0:T(2,128)} %bitcast.67) | data formatting | bytes 12582912
  246.0 0.8 constant_dynamic-update-slice_fusion.31
  246.9 1.8 constant_dynamic-update-slice_fusion.30
  248.6 1.8 constant_dynamic-update-slice_fusion.29
  250.4 1.8 constant_dynamic-update-slice_fusion.28
  252.2 1.8 constant_dynamic-update-slice_fusion.27
  254.0 0.8 constant_dynamic-update-slice_fusion.26
  254.8 10.2 %multiply_convert_fusion.1 = bf16[2048,768]{1,0:T(8,128)(2,1)S(1)} fusion(bf16[768,1536]{1,0:T(8,128)(2,1)S(1)} %bitcast.65, bf16[1,2048,1536]{2,1,0:T(8,128)(2,1)} %all-gather.4.cloned.1.call-done, f32[2048,768]{1,0:T(8,128)} %bitcast.70, f32[2048,768]{1,0:T(8,128)} %bitcast.68), kind=kOutput, calls=%fused_computation.11 | convolution fusion | flops 4836556800 | bytes 24379392 | tf_op jit(solution)/shard_map/dot_general | solution.py:68
  265.0 1.6 copy-done.29
  266.6 6.9 %convolution_convert_fusion = bf16[2048,1536]{1,0:T(8,128)(2,1)} fusion(bf16[2048,768]{1,0:T(8,128)(2,1)S(1)} %multiply_convert_fusion.1, bf16[1536,768]{0,1:T(8,128)(2,1)S(1)} %bitcast.72), kind=kOutput, calls=%fused_computation | convolution fusion | flops 4834983936 | bytes 11796480 | tf_op jit(solution)/shard_map/dot_general | solution.py:70
  273.6 1.9 constant_dynamic-update-slice_fusion.25
  275.5 0.8 constant_dynamic-update-slice_fusion.24
  276.3 0.8 constant_dynamic-update-slice_fusion.23
  277.1 0.8 constant_dynamic-update-slice_fusion.22
  277.9 0.8 constant_dynamic-update-slice_fusion.21
  278.6 0.8 constant_dynamic-update-slice_fusion.20
  279.4 0.8 constant_dynamic-update-slice_fusion.19
  280.2 0.8 constant_dynamic-update-slice_fusion.18
  281.0 0.8 constant_dynamic-update-slice_fusion.17
  281.8 0.8 constant_dynamic-update-slice_fusion.16
  282.6 1.8 constant_dynamic-update-slice_fusion.15
  284.4 1.8 constant_dynamic-update-slice_fusion.14
  286.2 1.8 constant_dynamic-update-slice_fusion.13
  288.0 1.8 constant_dynamic-update-slice_fusion.12
  289.9 1.8 constant_dynamic-update-slice_fusion.11
  291.7 1.8 constant_dynamic-update-slice_fusion.10
  293.5 0.8 constant_dynamic-update-slice_fusion.9
  294.3 0.8 constant_dynamic-update-slice_fusion.8
  295.8 0.8 constant_dynamic-update-slice_fusion.6
  296.6 0.8 constant_dynamic-update-slice_fusion.5
  297.4 1.9 constant_dynamic-update-slice_fusion.4
  299.3 1.8 constant_dynamic-update-slice_fusion.3
  301.8 0.8 constant_dynamic-update-slice_fusion.1
  302.6 0.8 constant_dynamic-update-slice_fusion
  303.4 6.9 %fusion.32 = bf16[1,1,1536,384]{3,2,1,0:T(8,128)(2,1)S(1)} fusion(bf16[4096,1536]{1,0:T(8,128)(2,1)} %constant_dynamic-update-slice_fusion, s32[]{:T(128)S(6)} %select_n.29, bf16[2048,768]{1,0:T(8,128)(2,1)S(1)} %copy-done.30), kind=kOutput, calls=%fused_computation.26 | convolution fusion | flops 2416508928 | bytes 9043972 | tf_op jit(solution)/shard_map/dot_general | solution.py:76
  310.4 29.3 %fusion.16 = bf16[768,1536]{1,0:T(8,128)(2,1)} fusion(bf16[1,2048,1536]{2,1,0:T(8,128)(2,1)} %all-gather.4.cloned.1.call-done, bf16[1536,768]{0,1:T(8,128)(2,1)S(1)} %bitcast.73, bf16[4096,1536]{1,0:T(8,128)(2,1)} %constant_dynamic-update-slice_fusion, s32[]{:T(128)S(6)} %select_n.29, f32[2048,768]{1,0:T(8,128)} %bitcast.71, f32[2048,768]{1,0:T(8,128)} %bitcast.69), kind=kOutput, calls=%fused_computation.20 | convolution fusion | flops 9669574656 | bytes 29884420 | tf_op jit(solution)/shard_map/dot_general | solution.py:73
  339.7 20.6 %reduce-scatter.2.cloned.1.call-done = bf16[128,1536]{1,0:T(8,128)(2,1)} async-done(((bf16[2048,1536]{1,0:T(8,128)(2,1)}), bf16[128,1536]{1,0:T(8,128)(2,1)}) %reduce-scatter.2.cloned.1.call-update) | async-done | bytes 393232 | tf_op jit(solution)/shard_map/reduce_scatter | solution.py:71
  360.3 1.4 collective-permute-start.1
  361.7 6.7 %fusion.29 = bf16[1,1,1536,384]{3,2,1,0:T(8,128)(2,1)S(1)} fusion(bf16[4096,1536]{1,0:T(8,128)(2,1)} %constant_dynamic-update-slice_fusion, s32[]{:T(128)S(6)} %select_n.29, bf16[2048,768]{1,0:T(8,128)(2,1)} %copy-done.29), kind=kOutput, calls=%fused_computation.25 | convolution fusion | flops 2416508928 | bytes 9043972 | tf_op jit(solution)/shard_map/dot_general | solution.py:76
  368.4 1.7 pad_maximum_fusion
  (109 shorter events, 15.0 us)
Async XLA Ops:
  7.2 247.6 %copy-start = (bf16[1,2,384,1536]{3,2,1,0:T(8,128)(2,1)S(1)}, bf16[1,2,384,1536]{3,2,1,0:T(8,128)(2,1)}, u32[]{:S(2)}) copy-start(bf16[1,2,384,1536]{3,2,1,0:T(8,128)(2,1)} %param.13) | copy-start | bytes 7077892
  7.2 171.2 %copy-start.28 = (f32[1,128,8]{1,2,0:T(8,128)S(1)}, f32[1,128,8]{1,2,0:T(8,128)}, u32[]{:S(2)}) copy-start(f32[1,128,8]{1,2,0:T(8,128)} %param.11) | copy-start | bytes 12292
  7.2 247.6 %all-gather.4.cloned.1.call-start = ((), (), s32[]{:S(2)}) async-start(), calls=%async_computation.3 | async-start | bytes 6684672 | tf_op jit(solution)/shard_map/all_gather | solution.py:48
  7.2 12.4 %collective-permute-start = (bf16[1,128,1536]{2,1,0:T(8,128)(2,1)}, bf16[1,128,1536]{2,1,0:T(8,128)(2,1)S(1)}, u32[]{:S(2)}, u32[]{:S(2)}) collective-permute-start(bf16[1,128,1536]{2,1,0:T(8,128)(2,1)} %param.8), channel_id=1, source_target_pairs={{16,0},{0,16},{17,1},{1,17},{18,2},{2,18},{19,3},{3,19},{20,4},{4,... | collective-permute-start | bytes 1179656 | tf_op jit(solution)/shard_map/ppermute | solution.py:13
  19.6 0.7 copy-start.26
  20.4 10.2 %collective-permute-start.2 = (bf16[128,1536]{1,0:T(8,128)(2,1)}, bf16[128,1536]{1,0:T(8,128)(2,1)S(1)}, u32[]{:S(2)}, u32[]{:S(2)}) collective-permute-start(bf16[128,1536]{1,0:T(8,128)(2,1)} %bitcast.74), channel_id=1, source_target_pairs={{0,1},{1,2},{2,3},{3,4},{4,5},{5,6},{6,7},{7,8},{8,9},{9,10},{10,1... | collective-permute-start | bytes 1179656 | tf_op jit(solution)/shard_map/ppermute | solution.py:44
  30.6 0.7 copy-start.5
  31.3 18.3 %collective-permute-start.3 = (bf16[128,1536]{1,0:T(8,128)(2,1)S(1)}, bf16[128,1536]{1,0:T(8,128)(2,1)S(1)}, u32[]{:S(2)}, u32[]{:S(2)}) collective-permute-start(bf16[128,1536]{1,0:T(8,128)(2,1)S(1)} %collective-permute-done.2), channel_id=1, source_target_pairs={{0,1},{1,2},{2,3},{3,4},{4,5},{5,6},{6,7},{7,8},{8,9},{9,10},{10,1... | collective-permute-start | bytes 1179656 | tf_op jit(solution)/shard_map/ppermute | solution.py:44
  49.6 0.8 copy-start.7
  50.3 10.1 %collective-permute-start.4 = (bf16[128,1536]{1,0:T(8,128)(2,1)S(1)}, bf16[128,1536]{1,0:T(8,128)(2,1)S(1)}, u32[]{:S(2)}, u32[]{:S(2)}) collective-permute-start(bf16[128,1536]{1,0:T(8,128)(2,1)S(1)} %collective-permute-done.3), channel_id=1, source_target_pairs={{0,1},{1,2},{2,3},{3,4},{4,5},{5,6},{6,7},{7,8},{8,9},{9,10},{10,1... | collective-permute-start | bytes 1179656 | tf_op jit(solution)/shard_map/ppermute | solution.py:44
  60.4 0.8 copy-start.9
  61.2 18.4 %collective-permute-start.5 = (bf16[128,1536]{1,0:T(8,128)(2,1)S(1)}, bf16[128,1536]{1,0:T(8,128)(2,1)S(1)}, u32[]{:S(2)}, u32[]{:S(2)}) collective-permute-start(bf16[128,1536]{1,0:T(8,128)(2,1)S(1)} %collective-permute-done.4), channel_id=1, source_target_pairs={{0,1},{1,2},{2,3},{3,4},{4,5},{5,6},{6,7},{7,8},{8,9},{9,10},{10,1... | collective-permute-start | bytes 1179656 | tf_op jit(solution)/shard_map/ppermute | solution.py:44
  79.6 0.8 copy-start.11
  80.4 17.0 %collective-permute-start.6 = (bf16[128,1536]{1,0:T(8,128)(2,1)S(1)}, bf16[128,1536]{1,0:T(8,128)(2,1)S(1)}, u32[]{:S(2)}, u32[]{:S(2)}) collective-permute-start(bf16[128,1536]{1,0:T(8,128)(2,1)S(1)} %collective-permute-done.5), channel_id=1, source_target_pairs={{0,1},{1,2},{2,3},{3,4},{4,5},{5,6},{6,7},{7,8},{8,9},{9,10},{10,1... | collective-permute-start | bytes 1179656 | tf_op jit(solution)/shard_map/ppermute | solution.py:44
  97.4 0.7 copy-start.13
  98.1 9.9 %collective-permute-start.7 = (bf16[128,1536]{1,0:T(8,128)(2,1)S(1)}, bf16[128,1536]{1,0:T(8,128)(2,1)S(1)}, u32[]{:S(2)}, u32[]{:S(2)}) collective-permute-start(bf16[128,1536]{1,0:T(8,128)(2,1)S(1)} %collective-permute-done.6), channel_id=1, source_target_pairs={{0,1},{1,2},{2,3},{3,4},{4,5},{5,6},{6,7},{7,8},{8,9},{9,10},{10,1... | collective-permute-start | bytes 1179656 | tf_op jit(solution)/shard_map/ppermute | solution.py:44
  108.0 0.8 copy-start.15
  108.8 9.9 %collective-permute-start.8 = (bf16[128,1536]{1,0:T(8,128)(2,1)S(1)}, bf16[128,1536]{1,0:T(8,128)(2,1)S(1)}, u32[]{:S(2)}, u32[]{:S(2)}) collective-permute-start(bf16[128,1536]{1,0:T(8,128)(2,1)S(1)} %collective-permute-done.7), channel_id=1, source_target_pairs={{0,1},{1,2},{2,3},{3,4},{4,5},{5,6},{6,7},{7,8},{8,9},{9,10},{10,1... | collective-permute-start | bytes 1179656 | tf_op jit(solution)/shard_map/ppermute | solution.py:44
  118.7 92.6 %copy-start.17 = (bf16[128,1536]{1,0:T(8,128)(2,1)}, bf16[128,1536]{1,0:T(8,128)(2,1)S(1)}, u32[]{:S(2)}) copy-start(bf16[128,1536]{1,0:T(8,128)(2,1)S(1)} %collective-permute-done.8) | copy-start | bytes 1179652
  118.7 9.9 %collective-permute-start.9 = (bf16[128,1536]{1,0:T(8,128)(2,1)S(1)}, bf16[128,1536]{1,0:T(8,128)(2,1)S(1)}, u32[]{:S(2)}, u32[]{:S(2)}) collective-permute-start(bf16[128,1536]{1,0:T(8,128)(2,1)S(1)} %collective-permute-done.8), channel_id=1, source_target_pairs={{0,1},{1,2},{2,3},{3,4},{4,5},{5,6},{6,7},{7,8},{8,9},{9,10},{10,1... | collective-permute-start | bytes 1179656 | tf_op jit(solution)/shard_map/ppermute | solution.py:44
  128.6 82.7 %copy-start.19 = (bf16[128,1536]{1,0:T(8,128)(2,1)}, bf16[128,1536]{1,0:T(8,128)(2,1)S(1)}, u32[]{:S(2)}) copy-start(bf16[128,1536]{1,0:T(8,128)(2,1)S(1)} %collective-permute-done.9) | copy-start | bytes 1179652
  128.6 9.9 %collective-permute-start.10 = (bf16[128,1536]{1,0:T(8,128)(2,1)S(1)}, bf16[128,1536]{1,0:T(8,128)(2,1)S(1)}, u32[]{:S(2)}, u32[]{:S(2)}) collective-permute-start(bf16[128,1536]{1,0:T(8,128)(2,1)S(1)} %collective-permute-done.9), channel_id=1, source_target_pairs={{0,1},{1,2},{2,3},{3,4},{4,5},{5,6},{6,7},{7,8},{8,9},{9,10},{10,1... | collective-permute-start | bytes 1179656 | tf_op jit(solution)/shard_map/ppermute | solution.py:44
  132.7 91.2 %all-to-all-start = ((bf16[16,2,48,384]{3,2,1,0:T(8,128)(2,1)}), bf16[16,2,48,384]{3,2,1,0:T(8,128)(2,1)}, u32[]{:S(2)}, u32[]{:S(2)}) async-start(bf16[16,2,48,384]{3,2,1,0:T(8,128)(2,1)} %bitcast.75), calls=%async_computation | async-start | bytes 2359296 | tf_op jit(solution)/shard_map/all_to_all | solution.py:36
  138.4 221.9 %reduce-scatter.2.cloned.1.call-start = ((), (), s32[]{:S(2)}) async-start(), calls=%async_computation.2 | async-start | bytes 6684672 | tf_op jit(solution)/shard_map/reduce_scatter | solution.py:71
  138.5 72.8 %copy-start.21 = (bf16[128,1536]{1,0:T(8,128)(2,1)}, bf16[128,1536]{1,0:T(8,128)(2,1)S(1)}, u32[]{:S(2)}) copy-start(bf16[128,1536]{1,0:T(8,128)(2,1)S(1)} %collective-permute-done.10) | copy-start | bytes 1179652
  138.5 29.1 %collective-permute-start.11 = (bf16[128,1536]{1,0:T(8,128)(2,1)S(1)}, bf16[128,1536]{1,0:T(8,128)(2,1)S(1)}, u32[]{:S(2)}, u32[]{:S(2)}) collective-permute-start(bf16[128,1536]{1,0:T(8,128)(2,1)S(1)} %collective-permute-done.10), channel_id=1, source_target_pairs={{0,1},{1,2},{2,3},{3,4},{4,5},{5,6},{6,7},{7,8},{8,9},{9,10},{10,1... | collective-permute-start | bytes 1179656 | tf_op jit(solution)/shard_map/ppermute | solution.py:44
  167.6 0.8 copy-start.23
  168.4 10.0 %collective-permute-start.12 = (bf16[128,1536]{1,0:T(8,128)(2,1)S(1)}, bf16[128,1536]{1,0:T(8,128)(2,1)}, u32[]{:S(2)}, u32[]{:S(2)}) collective-permute-start(bf16[128,1536]{1,0:T(8,128)(2,1)S(1)} %collective-permute-done.11), channel_id=1, source_target_pairs={{0,1},{1,2},{2,3},{3,4},{4,5},{5,6},{6,7},{7,8},{8,9},{9,10},{10,1... | collective-permute-start | bytes 1179656 | tf_op jit(solution)/shard_map/ppermute | solution.py:44
  178.4 20.0 %collective-permute-start.13 = (bf16[128,1536]{1,0:T(8,128)(2,1)}, bf16[128,1536]{1,0:T(8,128)(2,1)}, u32[]{:S(2)}, u32[]{:S(2)}) collective-permute-start(bf16[128,1536]{1,0:T(8,128)(2,1)} %collective-permute-done.12), channel_id=1, source_target_pairs={{0,1},{1,2},{2,3},{3,4},{4,5},{5,6},{6,7},{7,8},{8,9},{9,10},{10,1... | collective-permute-start | bytes 1179656 | tf_op jit(solution)/shard_map/ppermute | solution.py:44
  198.4 10.3 %collective-permute-start.14 = (bf16[128,1536]{1,0:T(8,128)(2,1)}, bf16[128,1536]{1,0:T(8,128)(2,1)}, u32[]{:S(2)}, u32[]{:S(2)}) collective-permute-start(bf16[128,1536]{1,0:T(8,128)(2,1)} %collective-permute-done.13), channel_id=1, source_target_pairs={{0,1},{1,2},{2,3},{3,4},{4,5},{5,6},{6,7},{7,8},{8,9},{9,10},{10,1... | collective-permute-start | bytes 1179656 | tf_op jit(solution)/shard_map/ppermute | solution.py:44
  208.7 15.2 %collective-permute-start.15 = (bf16[128,1536]{1,0:T(8,128)(2,1)}, bf16[128,1536]{1,0:T(8,128)(2,1)}, u32[]{:S(2)}, u32[]{:S(2)}) collective-permute-start(bf16[128,1536]{1,0:T(8,128)(2,1)} %collective-permute-done.14), channel_id=1, source_target_pairs={{0,1},{1,2},{2,3},{3,4},{4,5},{5,6},{6,7},{7,8},{8,9},{9,10},{10,1... | collective-permute-start | bytes 1179656 | tf_op jit(solution)/shard_map/ppermute | solution.py:44
  211.7 12.2 %copy-start.27 = (f32[16,128,2]{1,2,0:T(2,128)S(1)}, f32[16,128,2]{1,2,0:T(2,128)}, u32[]{:S(2)}) copy-start(f32[16,128,2]{1,2,0:T(2,128)} %copy.37) | copy-start | bytes 49156
  223.9 22.2 %collective-permute-start.16 = (bf16[128,1536]{1,0:T(8,128)(2,1)}, bf16[128,1536]{1,0:T(8,128)(2,1)S(1)}, u32[]{:S(2)}, u32[]{:S(2)}) collective-permute-start(bf16[128,1536]{1,0:T(8,128)(2,1)} %collective-permute-done.15), channel_id=1, source_target_pairs={{0,1},{1,2},{2,3},{3,4},{4,5},{5,6},{6,7},{7,8},{8,9},{9,10},{10,1... | collective-permute-start | bytes 1179656 | tf_op jit(solution)/shard_map/ppermute | solution.py:44
  229.7 24.3 %copy-start.24 = (bf16[128,1536]{1,0:T(8,128)(2,1)S(1)}, bf16[128,1536]{1,0:T(8,128)(2,1)}, u32[]{:S(2)}) copy-start(bf16[128,1536]{1,0:T(8,128)(2,1)} %copy-done.23) | copy-start | bytes 1179652
  246.0 18.9 %copy-start.25 = (bf16[128,1536]{1,0:T(8,128)(2,1)}, bf16[128,1536]{1,0:T(8,128)(2,1)S(1)}, u32[]{:S(2)}) copy-start(bf16[128,1536]{1,0:T(8,128)(2,1)S(1)} %collective-permute-done.16) | copy-start | bytes 1179652
  254.7 11.8 %copy-start.2 = (bf16[1,2,1536,384]{2,3,1,0:T(8,128)(2,1)S(1)}, bf16[1,2,1536,384]{2,3,1,0:T(8,128)(2,1)}, u32[]{:S(2)}) copy-start(bf16[1,2,1536,384]{2,3,1,0:T(8,128)(2,1)} %copy.42) | copy-start | bytes 7077892
  264.9 1.6 copy-start.29
  266.6 9.0 %copy-start.20 = (bf16[128,1536]{1,0:T(8,128)(2,1)S(1)}, bf16[128,1536]{1,0:T(8,128)(2,1)}, u32[]{:S(2)}) copy-start(bf16[128,1536]{1,0:T(8,128)(2,1)} %copy-done.19) | copy-start | bytes 1179652
  266.6 9.8 %copy-start.18 = (bf16[128,1536]{1,0:T(8,128)(2,1)S(1)}, bf16[128,1536]{1,0:T(8,128)(2,1)}, u32[]{:S(2)}) copy-start(bf16[128,1536]{1,0:T(8,128)(2,1)} %copy-done.17) | copy-start | bytes 1179652
  266.6 10.5 %copy-start.16 = (bf16[128,1536]{1,0:T(8,128)(2,1)S(1)}, bf16[128,1536]{1,0:T(8,128)(2,1)}, u32[]{:S(2)}) copy-start(bf16[128,1536]{1,0:T(8,128)(2,1)} %copy-done.15) | copy-start | bytes 1179652
  266.6 11.3 %copy-start.14 = (bf16[128,1536]{1,0:T(8,128)(2,1)S(1)}, bf16[128,1536]{1,0:T(8,128)(2,1)}, u32[]{:S(2)}) copy-start(bf16[128,1536]{1,0:T(8,128)(2,1)} %copy-done.13) | copy-start | bytes 1179652
  266.6 12.1 %copy-start.12 = (bf16[128,1536]{1,0:T(8,128)(2,1)S(1)}, bf16[128,1536]{1,0:T(8,128)(2,1)}, u32[]{:S(2)}) copy-start(bf16[128,1536]{1,0:T(8,128)(2,1)} %copy-done.11) | copy-start | bytes 1179652
  266.6 12.8 %copy-start.10 = (bf16[128,1536]{1,0:T(8,128)(2,1)S(1)}, bf16[128,1536]{1,0:T(8,128)(2,1)}, u32[]{:S(2)}) copy-start(bf16[128,1536]{1,0:T(8,128)(2,1)} %copy-done.9) | copy-start | bytes 1179652
  266.6 13.6 %copy-start.8 = (bf16[128,1536]{1,0:T(8,128)(2,1)S(1)}, bf16[128,1536]{1,0:T(8,128)(2,1)}, u32[]{:S(2)}) copy-start(bf16[128,1536]{1,0:T(8,128)(2,1)} %copy-done.7) | copy-start | bytes 1179652
  273.5 7.5 %copy-start.6 = (bf16[128,1536]{1,0:T(8,128)(2,1)S(1)}, bf16[128,1536]{1,0:T(8,128)(2,1)}, u32[]{:S(2)}) copy-start(bf16[128,1536]{1,0:T(8,128)(2,1)} %copy-done.5) | copy-start | bytes 1179652
  273.5 8.3 %copy-start.4 = (bf16[1,128,1536]{2,1,0:T(8,128)(2,1)S(1)}, bf16[1,128,1536]{2,1,0:T(8,128)(2,1)}, u32[]{:S(2)}) copy-start(bf16[1,128,1536]{2,1,0:T(8,128)(2,1)} %param.7) | copy-start | bytes 1179652
  273.6 20.0 %copy-start.22 = (bf16[128,1536]{1,0:T(8,128)(2,1)S(1)}, bf16[128,1536]{1,0:T(8,128)(2,1)}, u32[]{:S(2)}) copy-start(bf16[128,1536]{1,0:T(8,128)(2,1)} %copy-done.21) | copy-start | bytes 1179652
  273.6 29.9 %copy-start.30 = (bf16[2048,768]{1,0:T(8,128)(2,1)S(1)}, bf16[2048,768]{1,0:T(8,128)(2,1)}, u32[]{:S(2)}) copy-start(bf16[2048,768]{1,0:T(8,128)(2,1)} %copy-done.29) | copy-start | bytes 9437188
  297.4 13.0 %copy-start.3 = (bf16[1,2,1536,384]{2,3,1,0:T(8,128)(2,1)S(1)}, bf16[1,2,1536,384]{2,3,1,0:T(8,128)(2,1)}, u32[]{:S(2)}) copy-start(bf16[1,2,1536,384]{2,3,1,0:T(8,128)(2,1)} %copy.42) | copy-start | bytes 7077892
  360.3 11.1 %copy-start.1 = (bf16[1,2,384,1536]{3,2,1,0:T(8,128)(2,1)S(1)}, bf16[1,2,384,1536]{3,2,1,0:T(8,128)(2,1)}, u32[]{:S(2)}) copy-start(bf16[1,2,384,1536]{3,2,1,0:T(8,128)(2,1)} %param.13) | copy-start | bytes 7077892
  360.3 10.3 %collective-permute-start.1 = (bf16[1,128,1536]{2,1,0:T(8,128)(2,1)}, bf16[1,128,1536]{2,1,0:T(8,128)(2,1)S(1)}, u32[]{:S(2)}, u32[]{:S(2)}) collective-permute-start(bf16[1,128,1536]{2,1,0:T(8,128)(2,1)} %bitcast.82), channel_id=1, source_target_pairs={{16,0},{0,16},{17,1},{1,17},{18,2},{2,18},{19,3},{3,19},{20,4},{4,... | collective-permute-start | bytes 1179656 | tf_op jit(solution)/shard_map/ppermute | solution.py:13
Sparse Core Ops, SparseCore 0:
  20.5 71.2 all-gather.3
  273.7 86.5 reduce-scatter.1
